TPU v7x, 32 devices: a whole 2x2x4 slice. The times are simulated.
32 devices in a mesh: groups: 2 (over y), band: 4 (over z), chan: 4 (over x, core).
Axes of the slice: x: 2, y: 2, z: 4, core: 2. Of those that a mesh axis runs over, the one named last changes fastest.
Arguments:
- slide_region: float32 [16, 32, 8192], P('chan', ('groups', 'band')), parts along dimension 1, may hold values from -6 to 6
- row_taps: float32 [16, 257], P('chan'), may hold values from -0.375 to 0.375
- column_taps: float32 [16, 257], replicated, may hold values from -0.375 to 0.375
- channel_mix: float32 [16, 16], replicated, may hold values from -1.5 to 1.5
Outputs:
- filtered: float32 [16, 32, 8192], P('chan', ('groups', 'band')), parts along dimension 1
There are 2 independent parts, one for each index of `groups`. A program takes and returns all parts, laid end to end along the dimension named above; an argument that names none is the same for every part. Nothing has to cross between parts.
All inputs are finite; a program needn't handle non-finite values.
Results may differ from a plain program's by a relative error of at most 0.00007.
Values sent between devices are 32-bit elements; how exact they have to be, the bound alone decides.
A program may use at most 64 MiB of HBM per device.

v0:
```python
import functools

import jax
import jax.numpy as jnp
from jax import lax
from jax.experimental import pallas as pl
from jax.experimental.pallas import tpu as pltpu
from jax.sharding import PartitionSpec as P

precise = lax.Precision.HIGHEST


def band_tables(filter_taps, tile_size):
    channels, length = filter_taps.shape
    margin = (length - 1) // 2
    period = 4 * tile_size
    border = 3 * tile_size + length
    widened = jnp.pad(filter_taps, ((0, 0), (border, border)))
    lowest = margin - tile_size + border
    window = widened[:, lowest : lowest + 3 * tile_size]
    vector = jnp.pad(window, ((0, 0), (0, tile_size)))
    repeated = jnp.tile(vector, (1, tile_size))[:, : tile_size * (period - 1)]
    toeplitz = repeated.reshape(channels, tile_size, period - 1)[:, :, : 3 * tile_size]
    stacked = jnp.transpose(toeplitz, (0, 2, 1))
    return stacked.reshape(channels, 3, tile_size, tile_size)


def along_columns(signal, filter_taps):
    tile_size = 128
    tables = band_tables(filter_taps, tile_size)
    channels, row_count, col_count = signal.shape
    tile_count = col_count // tile_size
    tiled = signal.reshape(channels, row_count, tile_count, tile_size)
    padded = jnp.pad(tiled, ((0, 0), (0, 0), (1, 1), (0, 0)))
    result = jnp.einsum(
        "crti,cij->crtj", padded[:, :, 0:tile_count], tables[:, 0], precision=precise
    )
    result = result + jnp.einsum(
        "crti,cij->crtj", padded[:, :, 1 : tile_count + 1], tables[:, 1], precision=precise
    )
    result = result + jnp.einsum(
        "crti,cij->crtj", padded[:, :, 2:], tables[:, 2], precision=precise
    )
    return result.reshape(channels, row_count, col_count)


def along_rows(signal, filter_taps):
    channels, row_count, col_count = signal.shape
    tile_size = 128 if row_count % 128 == 0 else row_count
    tables = band_tables(filter_taps, tile_size)
    tile_count = row_count // tile_size
    tiled = signal.reshape(channels, tile_count, tile_size, col_count)
    padded = jnp.pad(tiled, ((0, 0), (1, 1), (0, 0), (0, 0)))
    result = jnp.einsum("ctiw,cij->ctjw", padded[:, 0:tile_count], tables[:, 0], precision=precise)
    result = result + jnp.einsum(
        "ctiw,cij->ctjw", padded[:, 1 : tile_count + 1], tables[:, 1], precision=precise
    )
    result = result + jnp.einsum("ctiw,cij->ctjw", padded[:, 2:], tables[:, 2], precision=precise)
    return result.reshape(channels, row_count, col_count)


def on_device(slide_region, row_taps, column_taps, channel_mix):
    local_channels = slide_region.shape[0]
    across = along_columns(slide_region, row_taps)
    column_band = lax.all_to_all(across, "band", split_axis=2, concat_axis=1, tiled=True)
    first_channel = lax.axis_index("chan") * local_channels
    own_taps = lax.dynamic_slice_in_dim(column_taps, first_channel, local_channels, 0)
    vertical = along_rows(column_band, own_taps)
    own_mixing = lax.dynamic_slice_in_dim(channel_mix, first_channel, local_channels, 0)
    blended = jnp.einsum(
        "oc,chw->ohw",
        own_mixing,
        lax.all_gather(vertical, "chan", axis=0, tiled=True),
        precision=precise,
    )
    return lax.all_to_all(blended, "band", split_axis=1, concat_axis=2, tiled=True)


LANES = 128
CHUNKS = 2


def split(value):
    high = value.astype(jnp.bfloat16)
    return high, (value - high.astype(jnp.float32)).astype(jnp.bfloat16)


def product(left, right, dims):
    (left_high, left_low), (right_high, right_low) = left, right
    dot = functools.partial(
        lax.dot_general, dimension_numbers=(dims, ((), ())), preferred_element_type=jnp.float32
    )
    return dot(left_high, right_high) + (dot(left_low, right_high) + dot(left_high, right_low))


def filter_table(taps):
    shape = (LANES, LANES)
    lane = lax.broadcasted_iota(jnp.int32, shape, 1)
    row = lax.broadcasted_iota(jnp.int32, shape, 0)
    first, second = (
        pltpu.roll(
            jnp.broadcast_to(taps[:, at : at + LANES], shape), 0, 1, stride=1, stride_axis=0
        )
        for at in (0, LANES)
    )
    last = jnp.broadcast_to(taps[:, 2 * LANES :], shape)
    zero = jnp.zeros(shape, jnp.float32)
    return jnp.concatenate(
        [
            jnp.where(lane >= row, first, zero),
            jnp.where(lane >= row, second, first),
            jnp.where(lane == row, last, jnp.where(lane < row, second, zero)),
        ],
        axis=1,
    )


def mixing_table(column_taps, channel_mix, chans, bands, local_channels, local_rows):
    channels = chans * local_channels
    height = bands * local_rows
    block = local_channels * local_rows
    size = chans * bands * block
    margin = (column_taps.shape[1] - 1) // 2

    def coordinates(index):
        device, inner = index // block, index % block
        return (
            local_channels * (device % chans) + inner // local_rows,
            local_rows * (device // chans) + inner % local_rows,
        )

    tall = (size, channels)
    wide = (channels, size)
    pick_tall = (
        coordinates(lax.broadcasted_iota(jnp.int32, tall, 0))[0]
        == lax.broadcasted_iota(jnp.int32, tall, 1)
    ).astype(jnp.float32)
    pick_wide = (
        coordinates(lax.broadcasted_iota(jnp.int32, wide, 1))[0]
        == lax.broadcasted_iota(jnp.int32, wide, 0)
    ).astype(jnp.float32)
    weights = jnp.dot(
        jnp.dot(pick_tall, channel_mix, precision=precise), pick_wide, precision=precise
    )
    taps = lax.dot_general(
        column_taps[:, : 2 * margin],
        pick_wide,
        (((0,), (0,)), ((), ())),
        precision=precise,
    )
    square = (size, size)
    apart = (
        coordinates(lax.broadcasted_iota(jnp.int32, square, 1))[1]
        - coordinates(lax.broadcasted_iota(jnp.int32, square, 0))[1]
    )
    spread = jnp.zeros(square, jnp.float32)
    for distance in range(1 - height, height):
        at = margin + distance
        spread = jnp.where(apart == distance, taps[at : at + 1, :], spread)
    return weights * spread


def fused_kernel(
    chans, bands, x_hbm, row_taps, column_taps, channel_mix, out_ref,
    x_buf, tables, send_one, recv_one, send_two, mixing,
    ready, in_sem, send_one_sem, recv_one_sem, send_two_sem, recv_two_sem,
):
    local_channels, x_rows, _ = x_hbm.shape
    devices, _, block_rows, _ = send_two.shape
    tiles = send_one.shape[1]
    local_rows = block_rows // tiles
    chan, band = lax.axis_index("chan"), lax.axis_index("band")
    me = band * chans + chan

    half = bands // 2
    x_half = x_rows // 2
    peers = []
    for band_step in sorted(range(bands), key=lambda step: (step < half, step)):
        for chan_step in range(chans):
            if band_step or chan_step:
                to_chan, to_band = chan ^ chan_step, band ^ band_step
                slot = to_band * chans + to_chan
                name = {"chan": to_chan, "band": to_band}
                peers.append((name, slot))

    def each_peer(visit, also=None):
        for name, slot in peers:
            if also is None:
                visit(name, slot)
            else:
                pl.when(also(slot))(functools.partial(visit, name, slot))

    barrier = pltpu.get_barrier_semaphore()
    greet = functools.partial(
        pl.semaphore_signal, inc=1, device_id_type=pl.DeviceIdType.MESH
    )
    each_peer(lambda name, slot: greet(barrier, device_id=name), lambda slot: slot > me)
    loads = [
        pltpu.make_async_copy(x_hbm.at[c], x_buf.at[c, pl.ds(8, x_rows)], in_sem.at[c])
        for c in range(local_channels)
    ]
    for load in loads:
        load.start()

    @pl.when(me > 0)
    def _():
        pl.semaphore_wait(barrier, me)

    each_peer(lambda name, slot: greet(ready.at[me], device_id=name), lambda slot: slot < me)

    edge = jnp.zeros((8, LANES), jnp.float32)
    for c in range(local_channels):
        x_buf[c, 0:8, :] = edge
        x_buf[c, x_rows + 8 : x_rows + 16, :] = edge
        tables[c, 0], tables[c, 1] = split(filter_table(row_taps[c : c + 1, :]))

    def filter_half(which, first):
        start = pl.multiple_of(which * x_half, 8)
        for c in range(local_channels):
            if first:
                loads[c].wait()
            wide = x_buf[c, pl.ds(start, x_half + 16), :]
            window = jnp.concatenate(
                [
                    wide[8 + (k - 1) * local_rows : 8 + (k - 1) * local_rows + x_half]
                    for k in range(3)
                ],
                axis=1,
            )
            filtered = product(split(window), (tables[c, 0], tables[c, 1]), ((1,), (1,)))
            for device in range(devices // 2):
                for tile in range(tiles):
                    at = (device * tiles + tile) * local_rows
                    send_one[
                        which * (devices // 2) + device,
                        tile,
                        c * local_rows : (c + 1) * local_rows,
                        :,
                    ] = filtered[at : at + local_rows, :]

    step = tiles // CHUNKS

    def copy_one(chunk, name, slot):
        part = pl.ds(chunk * step, step)
        return pltpu.make_async_remote_copy(
            src_ref=send_one.at[slot, part],
            dst_ref=recv_one.at[part, me],
            send_sem=send_one_sem.at[chunk, slot],
            recv_sem=recv_one_sem.at[chunk, me],
            device_id=name,
            device_id_type=pl.DeviceIdType.MESH,
        )

    def send_one_to(chunk, name, slot):
        if chunk == 0:

            @pl.when(slot > me)
            def _():
                pl.semaphore_wait(ready.at[slot], 1)

        copy_one(chunk, name, slot).start()

    filter_half(1 - band // half, True)
    far = half * chans
    for name, slot in peers[:far]:
        send_one_to(0, name, slot)
    filter_half(band // half, False)
    for name, slot in peers[far:]:
        send_one_to(0, name, slot)
    for name, slot in peers:
        send_one_to(1, name, slot)
    recv_one[:, me] = send_one[me]

    table = mixing_table(
        column_taps[...], channel_mix[...], chans, bands, local_channels, local_rows
    )
    mixing[0], mixing[1] = split(table)

    rows = step * local_rows

    def copy_two(chunk, name, slot):
        return pltpu.make_async_remote_copy(
            src_ref=send_two.at[slot, :, pl.ds(chunk * rows, rows)],
            dst_ref=out_ref.at[
                :, pl.ds(pl.multiple_of(me * block_rows + chunk * rows, 8), rows)
            ],
            send_sem=send_two_sem.at[chunk, slot],
            recv_sem=recv_two_sem.at[chunk, me],
            device_id=name,
            device_id_type=pl.DeviceIdType.MESH,
        )

    for chunk in range(CHUNKS):
        part = pl.ds(chunk * step, step)
        def landed_one(name, slot):
            landed = recv_one.at[part, slot]
            pltpu.make_async_copy(landed, landed, recv_one_sem.at[chunk, slot]).wait()

        each_peer(landed_one)
        columns = jnp.concatenate(
            [
                recv_one[chunk * step + tile].reshape(mixing.shape[1], LANES)
                for tile in range(step)
            ],
            axis=1,
        )
        mixed = product((mixing[0], mixing[1]), split(columns), ((1,), (0,)))
        for device in range(devices):
            for c in range(local_channels):
                at = (device * local_channels + c) * local_rows
                for tile in range(step):
                    to = (chunk * step + tile) * local_rows
                    send_two[device, c, to : to + local_rows, :] = mixed[
                        at : at + local_rows, tile * LANES : (tile + 1) * LANES
                    ]
        there = pl.ds(pl.multiple_of(me * block_rows + chunk * rows, 8), rows)
        each_peer(lambda name, slot: copy_two(chunk, name, slot).start())
        out_ref[:, there, :] = send_two[me, :, chunk * rows : (chunk + 1) * rows, :]

    def finish(chunk, name, slot):
        landed = out_ref.at[
            :, pl.ds(pl.multiple_of(slot * block_rows + chunk * rows, 8), rows)
        ]
        pltpu.make_async_copy(landed, landed, recv_two_sem.at[chunk, slot]).wait()
        copy_one(chunk, name, slot).wait_send()
        copy_two(chunk, name, slot).wait_send()

    for chunk in range(CHUNKS):
        each_peer(functools.partial(finish, chunk))


def fused(chans, bands, slide_region, row_taps, column_taps, channel_mix):
    local_channels, local_rows, width = slide_region.shape
    devices = chans * bands
    total_tiles = width // LANES
    tiles = total_tiles // devices
    block = local_channels * local_rows
    tiled = slide_region.reshape(local_channels, local_rows, total_tiles, LANES)
    tiled = tiled.transpose(0, 2, 1, 3).reshape(local_channels, total_tiles * local_rows, LANES)
    vmem = pl.BlockSpec(memory_space=pltpu.VMEM)
    anywhere = pl.BlockSpec(memory_space=pl.ANY)
    dma = pltpu.SemaphoreType.DMA
    out = pl.pallas_call(
        functools.partial(fused_kernel, chans, bands),
        out_shape=pltpu.VMEM(tiled.shape, jnp.float32),
        in_specs=[anywhere, vmem, vmem, vmem],
        out_specs=vmem,
        scratch_shapes=[
            pltpu.VMEM((local_channels, tiled.shape[1] + 16, LANES), jnp.float32),
            pltpu.VMEM((local_channels, 2, LANES, 3 * LANES), jnp.bfloat16),
            pltpu.VMEM((devices, tiles, block, LANES), jnp.float32),
            pltpu.VMEM((tiles, devices, block, LANES), jnp.float32),
            pltpu.VMEM((devices, local_channels, tiles * local_rows, LANES), jnp.float32),
            pltpu.VMEM((2, devices * block, devices * block), jnp.bfloat16),
            pltpu.SemaphoreType.REGULAR((devices,)),
            dma((local_channels,)),
            dma((CHUNKS, devices)),
            dma((CHUNKS, devices)),
            dma((CHUNKS, devices)),
            dma((CHUNKS, devices)),
        ],
        compiler_params=pltpu.CompilerParams(collective_id=0, has_side_effects=True),
    )(tiled, row_taps, column_taps, channel_mix)
    out = out.reshape(local_channels, total_tiles, local_rows, LANES)
    return out.transpose(0, 2, 1, 3).reshape(slide_region.shape)


def power_of_two(number):
    return number & (number - 1) == 0


def program(chans, bands, slide_region, row_taps, column_taps, channel_mix):
    local_channels, local_rows, width = slide_region.shape
    devices = chans * bands
    margin = (row_taps.shape[1] - 1) // 2
    fits = (
        power_of_two(chans)
        and power_of_two(bands)
        and bands > 1
        and width % (devices * LANES * CHUNKS) == 0
        and margin == LANES
        and column_taps.shape[1] == row_taps.shape[1]
        and local_rows == 4
        and local_rows * bands <= margin
        and local_channels * local_rows % 8 == 0
        and width // (devices * LANES * CHUNKS) * local_rows % 8 == 0
        and devices * local_channels * local_rows <= 512
    )
    if fits:
        return fused(chans, bands, slide_region, row_taps, column_taps, channel_mix)
    return on_device(slide_region, row_taps, column_taps, channel_mix)


def solution(mesh):
    in_specs = (P("chan", ("groups", "band"), None), P("chan", None), P(), P())
    out_specs = P("chan", ("groups", "band"), None)
    return jax.shard_map(
        functools.partial(program, mesh.shape["chan"], mesh.shape["band"]),
        mesh=mesh,
        in_specs=in_specs,
        out_specs=out_specs,
        check_vma=False,
    )
```

profile of v0, /device:TPU:0, one launch (start us, length us, event | category | flops | bytes accessed | tf_op | source)
XLA Modules:
  0.0 31.9 jit_solution(11175018947560493434)
XLA Ops:
  0.0 31.0 %shard_map.46 = f32[4,256,128]{2,1,0:T(8,128)S(1)} custom-call(f32[4,256,128]{2,1,0:T(8,128)} %bitcast.11, f32[4,257]{1,0:T(4,128)} %row_taps.1, f32[16,257]{1,0:T(8,128)} %column_taps.1, f32[16,16]{1,0:T(8,128)} %channel_mix.1), custom_call_target="tpu_custom_call" | custom-call | tf_op jit(solution)/shard_map/pallas_call | solution.py:343
  31.1 0.8 %copy.8 = f32[4,4,8192]{2,1,0:T(4,128)} copy(f32[4,4,8192]{2,1,0:T(4,128)S(1)} %bitcast.10) | data formatting | bytes 1048576
where the time goes:
time: 32.1 us; the launch traced here: 31.9 us
  Pallas kernels  31 us (97%)
  local copies, waits for them, and re-layouts  0.8 us (2%)
    pallas_call x1, Pallas kernels, fused(): pl.pallas_call(functools.partial(fused_kernel, chans, bands), out_shape=p...  31 us
    unnamed x1, local copies, waits for them, and re-layouts  0.8 us

commit v1 on v0

--- a/solution.py
+++ b/solution.py
@@ -161,78 +161,99 @@
 
 
 def fused_kernel(
-    chans, bands, x_hbm, row_taps, column_taps, channel_mix, out_ref,
-    x_buf, tables, send_one, recv_one, send_two, mixing,
-    ready, in_sem, send_one_sem, recv_one_sem, send_two_sem, recv_two_sem,
+    chans, bands, x_hbm, row_hbm, column_hbm, mix_hbm, out_ref,
+    x_buf, row_taps, column_taps, channel_mix, tables,
+    send_one, recv_one, send_two, mixing,
+    ready, x_sem, row_sem, small_sem, send_sem, recv_one_sem, recv_two_sem,
 ):
     local_channels, x_rows, _ = x_hbm.shape
     devices, _, block_rows, _ = send_two.shape
     tiles = send_one.shape[1]
     local_rows = block_rows // tiles
+    band_rows = x_rows // bands
+    others = pl.ds(0, devices - 1)
     chan, band = lax.axis_index("chan"), lax.axis_index("band")
     me = band * chans + chan
-
     half = bands // 2
-    x_half = x_rows // 2
-    peers = []
-    for band_step in sorted(range(bands), key=lambda step: (step < half, step)):
-        for chan_step in range(chans):
-            if band_step or chan_step:
-                to_chan, to_band = chan ^ chan_step, band ^ band_step
-                slot = to_band * chans + to_chan
-                name = {"chan": to_chan, "band": to_band}
-                peers.append((name, slot))
-
-    def each_peer(visit, also=None):
-        for name, slot in peers:
-            if also is None:
-                visit(name, slot)
-            else:
-                pl.when(also(slot))(functools.partial(visit, name, slot))
+    left = band < half
+
+    row_load = pltpu.make_async_copy(row_hbm, row_taps, row_sem)
+    row_load.start()
+    x_inside = x_buf.at[:, pl.ds(8, x_rows)]
+    for c in range(local_channels):
+        pltpu.make_async_copy(x_hbm.at[c], x_inside.at[c], x_sem).start()
+
+    far = [jnp.where(left, half + k, half - 1 - k) for k in range(half)]
+    near = [jnp.where(left, 0, half) + (band + k) % half for k in range(1, half)]
+
+    def peers(to_band, own):
+        return [
+            ({"chan": chan ^ step, "band": to_band}, to_band * chans + (chan ^ step))
+            for step in range(1 if own else 0, chans)
+        ]
+
+    targets = [(to, peers(to, False)) for to in far + near] + [(band, peers(band, True))]
 
     barrier = pltpu.get_barrier_semaphore()
     greet = functools.partial(
         pl.semaphore_signal, inc=1, device_id_type=pl.DeviceIdType.MESH
     )
-    each_peer(lambda name, slot: greet(barrier, device_id=name), lambda slot: slot > me)
-    loads = [
-        pltpu.make_async_copy(x_hbm.at[c], x_buf.at[c, pl.ds(8, x_rows)], in_sem.at[c])
-        for c in range(local_channels)
+
+    def greet_all(semaphore, upward):
+        for to, names in targets[:-1]:
+
+            @pl.when((to > band) if upward else (to < band))
+            def _():
+                for name, _slot in names:
+                    greet(semaphore, device_id=name)
+
+        for name, slot in targets[-1][1]:
+
+            @pl.when((slot > me) if upward else (slot < me))
+            def _():
+                greet(semaphore, device_id=name)
+
+    greet_all(barrier, True)
+    small_loads = [
+        pltpu.make_async_copy(column_hbm, column_taps, small_sem.at[0]),
+        pltpu.make_async_copy(mix_hbm, channel_mix, small_sem.at[1]),
     ]
-    for load in loads:
+    for load in small_loads:
         load.start()
-
-    @pl.when(me > 0)
-    def _():
-        pl.semaphore_wait(barrier, me)
-
-    each_peer(lambda name, slot: greet(ready.at[me], device_id=name), lambda slot: slot < me)
 
     edge = jnp.zeros((8, LANES), jnp.float32)
     for c in range(local_channels):
         x_buf[c, 0:8, :] = edge
         x_buf[c, x_rows + 8 : x_rows + 16, :] = edge
+
+    @pl.when(me > 0)
+    def _():
+        pl.semaphore_wait(barrier, me)
+
+    greet_all(ready.at[band], False)
+
+    row_load.wait()
+    for c in range(local_channels):
         tables[c, 0], tables[c, 1] = split(filter_table(row_taps[c : c + 1, :]))
-
-    def filter_half(which, first):
-        start = pl.multiple_of(which * x_half, 8)
+    pltpu.make_async_copy(x_hbm, x_inside, x_sem).wait()
+
+    def filter_band(which):
+        start = pl.multiple_of(which * band_rows, 8)
         for c in range(local_channels):
-            if first:
-                loads[c].wait()
-            wide = x_buf[c, pl.ds(start, x_half + 16), :]
+            wide = x_buf[c, pl.ds(start, band_rows + 16), :]
             window = jnp.concatenate(
                 [
-                    wide[8 + (k - 1) * local_rows : 8 + (k - 1) * local_rows + x_half]
+                    wide[8 + (k - 1) * local_rows : 8 + (k - 1) * local_rows + band_rows]
                     for k in range(3)
                 ],
                 axis=1,
             )
             filtered = product(split(window), (tables[c, 0], tables[c, 1]), ((1,), (1,)))
-            for device in range(devices // 2):
+            for device in range(chans):
                 for tile in range(tiles):
                     at = (device * tiles + tile) * local_rows
                     send_one[
-                        which * (devices // 2) + device,
+                        which * chans + device,
                         tile,
                         c * local_rows : (c + 1) * local_rows,
                         :,
@@ -245,32 +266,31 @@
         return pltpu.make_async_remote_copy(
             src_ref=send_one.at[slot, part],
             dst_ref=recv_one.at[part, me],
-            send_sem=send_one_sem.at[chunk, slot],
-            recv_sem=recv_one_sem.at[chunk, me],
+            send_sem=send_sem.at[0],
+            recv_sem=recv_one_sem.at[chunk],
             device_id=name,
             device_id_type=pl.DeviceIdType.MESH,
         )
 
-    def send_one_to(chunk, name, slot):
-        if chunk == 0:
-
-            @pl.when(slot > me)
-            def _():
-                pl.semaphore_wait(ready.at[slot], 1)
-
-        copy_one(chunk, name, slot).start()
-
-    filter_half(1 - band // half, True)
-    far = half * chans
-    for name, slot in peers[:far]:
-        send_one_to(0, name, slot)
-    filter_half(band // half, False)
-    for name, slot in peers[far:]:
-        send_one_to(0, name, slot)
-    for name, slot in peers:
-        send_one_to(1, name, slot)
+    for to, names in targets:
+        own = to is band
+        filter_band(to)
+        above = (chans - 1 - chan) if own else chans
+
+        @pl.when((above > 0) if own else (to > band))
+        def _():
+            pl.semaphore_wait(ready.at[to], above)
+
+        for name, slot in names:
+            copy_one(0, name, slot).start()
+    for chunk in range(1, CHUNKS):
+        for to, names in targets:
+            for name, slot in names:
+                copy_one(chunk, name, slot).start()
     recv_one[:, me] = send_one[me]
 
+    for load in small_loads:
+        load.wait()
     table = mixing_table(
         column_taps[...], channel_mix[...], chans, bands, local_channels, local_rows
     )
@@ -284,19 +304,16 @@
             dst_ref=out_ref.at[
                 :, pl.ds(pl.multiple_of(me * block_rows + chunk * rows, 8), rows)
             ],
-            send_sem=send_two_sem.at[chunk, slot],
-            recv_sem=recv_two_sem.at[chunk, me],
+            send_sem=send_sem.at[1],
+            recv_sem=recv_two_sem,
             device_id=name,
             device_id_type=pl.DeviceIdType.MESH,
         )
 
     for chunk in range(CHUNKS):
         part = pl.ds(chunk * step, step)
-        def landed_one(name, slot):
-            landed = recv_one.at[part, slot]
-            pltpu.make_async_copy(landed, landed, recv_one_sem.at[chunk, slot]).wait()
-
-        each_peer(landed_one)
+        landed = recv_one.at[part, others]
+        pltpu.make_async_copy(landed, landed, recv_one_sem.at[chunk]).wait()
         columns = jnp.concatenate(
             [
                 recv_one[chunk * step + tile].reshape(mixing.shape[1], LANES)
@@ -314,19 +331,17 @@
                         at : at + local_rows, tile * LANES : (tile + 1) * LANES
                     ]
         there = pl.ds(pl.multiple_of(me * block_rows + chunk * rows, 8), rows)
-        each_peer(lambda name, slot: copy_two(chunk, name, slot).start())
+        for _to, names in targets:
+            for name, slot in names:
+                copy_two(chunk, name, slot).start()
         out_ref[:, there, :] = send_two[me, :, chunk * rows : (chunk + 1) * rows, :]
 
-    def finish(chunk, name, slot):
-        landed = out_ref.at[
-            :, pl.ds(pl.multiple_of(slot * block_rows + chunk * rows, 8), rows)
-        ]
-        pltpu.make_async_copy(landed, landed, recv_two_sem.at[chunk, slot]).wait()
-        copy_one(chunk, name, slot).wait_send()
-        copy_two(chunk, name, slot).wait_send()
-
-    for chunk in range(CHUNKS):
-        each_peer(functools.partial(finish, chunk))
+    sent = send_one.at[others]
+    pltpu.make_async_copy(sent, sent, send_sem.at[0]).wait()
+    sent = send_two.at[others]
+    pltpu.make_async_copy(sent, sent, send_sem.at[1]).wait()
+    landed = out_ref.at[:, pl.ds(0, (devices - 1) * block_rows)]
+    pltpu.make_async_copy(landed, landed, recv_two_sem).wait()
 
 
 def fused(chans, bands, slide_region, row_taps, column_taps, channel_mix):
@@ -343,21 +358,25 @@
     out = pl.pallas_call(
         functools.partial(fused_kernel, chans, bands),
         out_shape=pltpu.VMEM(tiled.shape, jnp.float32),
-        in_specs=[anywhere, vmem, vmem, vmem],
+        in_specs=[anywhere] * 4,
         out_specs=vmem,
         scratch_shapes=[
             pltpu.VMEM((local_channels, tiled.shape[1] + 16, LANES), jnp.float32),
+            pltpu.VMEM(row_taps.shape, jnp.float32),
+            pltpu.VMEM(column_taps.shape, jnp.float32),
+            pltpu.VMEM(channel_mix.shape, jnp.float32),
             pltpu.VMEM((local_channels, 2, LANES, 3 * LANES), jnp.bfloat16),
             pltpu.VMEM((devices, tiles, block, LANES), jnp.float32),
             pltpu.VMEM((tiles, devices, block, LANES), jnp.float32),
             pltpu.VMEM((devices, local_channels, tiles * local_rows, LANES), jnp.float32),
             pltpu.VMEM((2, devices * block, devices * block), jnp.bfloat16),
-            pltpu.SemaphoreType.REGULAR((devices,)),
-            dma((local_channels,)),
-            dma((CHUNKS, devices)),
-            dma((CHUNKS, devices)),
-            dma((CHUNKS, devices)),
-            dma((CHUNKS, devices)),
+            pltpu.SemaphoreType.REGULAR((bands,)),
+            dma,
+            dma,
+            dma((2,)),
+            dma((2,)),
+            dma((CHUNKS,)),
+            dma,
         ],
         compiler_params=pltpu.CompilerParams(collective_id=0, has_side_effects=True),
     )(tiled, row_taps, column_taps, channel_mix)

time: 32.1 us -> 30.8 us (0.960)
  Pallas kernels: 31 us -> 29.9 us
    pallas_call x1, Pallas kernels: 31 us -> 29.9 us  [fused(): pl.pallas_call(functools.partial(fused_kernel, chans, bands), out_shape=p...]
where the time goes in v1:
time: 30.8 us; the launch traced here: 30.7 us
  Pallas kernels  29.9 us (97%)
  local copies, waits for them, and re-layouts  0.8 us (3%)
    pallas_call x1, Pallas kernels, fused(): pl.pallas_call(functools.partial(fused_kernel, chans, bands), out_shape=p...  29.9 us
    unnamed x1, local copies, waits for them, and re-layouts  0.8 us

profile of v1, /device:TPU:0, one launch (start us, length us, event | category | flops | bytes accessed | tf_op | source)
XLA Modules:
  0.0 30.7 jit_solution(6966099084514838685)
XLA Ops:
  0.0 29.9 %shard_map.46 = f32[4,256,128]{2,1,0:T(8,128)S(1)} custom-call(f32[4,256,128]{2,1,0:T(8,128)} %bitcast.11, f32[4,257]{1,0:T(4,128)} %row_hbm.1, f32[16,257]{1,0:T(8,128)} %column_hbm.1, f32[16,16]{1,0:T(8,128)} %mix_hbm.1), custom_call_target="tpu_custom_call" | custom-call | tf_op jit(solution)/shard_map/pallas_call | solution.py:358
  29.9 0.8 %copy.8 = f32[4,4,8192]{2,1,0:T(4,128)} copy(f32[4,4,8192]{2,1,0:T(4,128)S(1)} %bitcast.10) | data formatting | bytes 1048576

commit v2 on v1

--- a/solution.py
+++ b/solution.py
@@ -193,6 +193,7 @@
         ]
 
     targets = [(to, peers(to, False)) for to in far + near] + [(band, peers(band, True))]
+    rising = [(to, peers(to, False)) for to in (jnp.where(left, half + k, k) for k in range(half))]
 
     barrier = pltpu.get_barrier_semaphore()
     greet = functools.partial(
@@ -234,7 +235,7 @@
 
     row_load.wait()
     for c in range(local_channels):
-        tables[c, 0], tables[c, 1] = split(filter_table(row_taps[c : c + 1, :]))
+        tables[c, 0:LANES], tables[c, LANES:] = split(filter_table(row_taps[c : c + 1, :]))
     pltpu.make_async_copy(x_hbm, x_inside, x_sem).wait()
 
     def filter_band(which):
@@ -248,7 +249,15 @@
                 ],
                 axis=1,
             )
-            filtered = product(split(window), (tables[c, 0], tables[c, 1]), ((1,), (1,)))
+            both = lax.dot_general(
+                jnp.concatenate(split(window), axis=0),
+                tables[c],
+                (((1,), (1,)), ((), ())),
+                preferred_element_type=jnp.float32,
+            )
+            filtered = both[:band_rows, :LANES] + (
+                both[band_rows:, :LANES] + both[:band_rows, LANES:]
+            )
             for device in range(chans):
                 for tile in range(tiles):
                     at = (device * tiles + tile) * local_rows
@@ -309,6 +318,33 @@
             device_id=name,
             device_id_type=pl.DeviceIdType.MESH,
         )
+
+    late = band == half
+
+    def send_rising(chunk):
+        last = chunk == CHUNKS - 1
+        for at, (_to, names) in enumerate(rising):
+            if at == 0:
+                for name, slot in names:
+                    copy_two(chunk, name, slot).start()
+                continue
+            if last:
+                @pl.when(late)
+                def _():
+                    for earlier in range(CHUNKS - 1):
+                        for name, slot in names[1:4]:
+                            copy_two(earlier, name, slot).start()
+
+                for name, slot in names:
+                    copy_two(chunk, name, slot).start()
+            else:
+                for name, slot in names[:1] + names[4:]:
+                    copy_two(chunk, name, slot).start()
+
+                @pl.when(jnp.logical_not(late))
+                def _():
+                    for name, slot in names[1:4]:
+                        copy_two(chunk, name, slot).start()
 
     for chunk in range(CHUNKS):
         part = pl.ds(chunk * step, step)
@@ -331,7 +367,8 @@
                         at : at + local_rows, tile * LANES : (tile + 1) * LANES
                     ]
         there = pl.ds(pl.multiple_of(me * block_rows + chunk * rows, 8), rows)
-        for _to, names in targets:
+        send_rising(chunk)
+        for _to, names in targets[half:]:
             for name, slot in names:
                 copy_two(chunk, name, slot).start()
         out_ref[:, there, :] = send_two[me, :, chunk * rows : (chunk + 1) * rows, :]
@@ -365,7 +402,7 @@
             pltpu.VMEM(row_taps.shape, jnp.float32),
             pltpu.VMEM(column_taps.shape, jnp.float32),
             pltpu.VMEM(channel_mix.shape, jnp.float32),
-            pltpu.VMEM((local_channels, 2, LANES, 3 * LANES), jnp.bfloat16),
+            pltpu.VMEM((local_channels, 2 * LANES, 3 * LANES), jnp.bfloat16),
             pltpu.VMEM((devices, tiles, block, LANES), jnp.float32),
             pltpu.VMEM((tiles, devices, block, LANES), jnp.float32),
             pltpu.VMEM((devices, local_channels, tiles * local_rows, LANES), jnp.float32),

time: 30.8 us -> 28.8 us (0.935)
  the two profiles are of different devices: /device:TPU:0 before, /device:TPU:15 now
where the time goes in v2:
time: 28.8 us; the launch traced here: 28.3 us
  Pallas kernels  27.5 us (95%)
  local copies, waits for them, and re-layouts  0.8 us (3%)
    pallas_call x1, Pallas kernels, fused(): pl.pallas_call(functools.partial(fused_kernel, chans, bands), out_shape=p...  27.5 us
    unnamed x1, local copies, waits for them, and re-layouts  0.8 us

profile of v2, /device:TPU:15, one launch (start us, length us, event | category | flops | bytes accessed | tf_op | source)
XLA Modules:
  0.0 28.3 jit_solution(8973431079918920925)
XLA Ops:
  0.0 27.5 %shard_map.46 = f32[4,256,128]{2,1,0:T(8,128)S(1)} custom-call(f32[4,256,128]{2,1,0:T(8,128)} %bitcast.11, f32[4,257]{1,0:T(4,128)} %row_hbm.1, f32[16,257]{1,0:T(8,128)} %column_hbm.1, f32[16,16]{1,0:T(8,128)} %mix_hbm.1), custom_call_target="tpu_custom_call" | custom-call | tf_op jit(solution)/shard_map/pallas_call | solution.py:395
  27.5 0.8 %copy.8 = f32[4,4,8192]{2,1,0:T(4,128)} copy(f32[4,4,8192]{2,1,0:T(4,128)S(1)} %bitcast.10) | data formatting | bytes 1048576

commit v3 on v2

--- a/solution.py
+++ b/solution.py
@@ -193,17 +193,25 @@
         ]
 
     targets = [(to, peers(to, False)) for to in far + near] + [(band, peers(band, True))]
-    rising = [(to, peers(to, False)) for to in (jnp.where(left, half + k, k) for k in range(half))]
+    rising = [
+        (to, [({"chan": jnp.int32(k), "band": to}, to * chans + k) for k in range(chans)])
+        for to in (jnp.where(left, half + k, k) for k in range(half))
+    ]
 
     barrier = pltpu.get_barrier_semaphore()
     greet = functools.partial(
         pl.semaphore_signal, inc=1, device_id_type=pl.DeviceIdType.MESH
     )
 
+    def rank(which):
+        return jnp.where(which < half, 2 * (half - 1 - which), 2 * (which - half) + 1)
+
+    mine = rank(band)
+
     def greet_all(semaphore, upward):
         for to, names in targets[:-1]:
 
-            @pl.when((to > band) if upward else (to < band))
+            @pl.when((rank(to) > mine) if upward else (rank(to) < mine))
             def _():
                 for name, _slot in names:
                     greet(semaphore, device_id=name)
@@ -227,11 +235,17 @@
         x_buf[c, 0:8, :] = edge
         x_buf[c, x_rows + 8 : x_rows + 16, :] = edge
 
-    @pl.when(me > 0)
-    def _():
-        pl.semaphore_wait(barrier, me)
-
-    greet_all(ready.at[band], False)
+    def meet():
+        below = mine * chans + chan
+
+        @pl.when(below > 0)
+        def _():
+            pl.semaphore_wait(barrier, below)
+
+        greet_all(ready.at[band], False)
+
+    meet_first = jnp.logical_and(2 * chan >= chans, band > 0)
+    pl.when(meet_first)(meet)
 
     row_load.wait()
     for c in range(local_channels):
@@ -284,9 +298,11 @@
     for to, names in targets:
         own = to is band
         filter_band(to)
+        if to is targets[0][0]:
+            pl.when(jnp.logical_not(meet_first))(meet)
         above = (chans - 1 - chan) if own else chans
 
-        @pl.when((above > 0) if own else (to > band))
+        @pl.when((above > 0) if own else (rank(to) > mine))
         def _():
             pl.semaphore_wait(ready.at[to], above)
 

time: 28.8 us -> 28.1 us (0.976)
  Pallas kernels: 27.5 us -> 26.8 us
    pallas_call x1, Pallas kernels: 27.5 us -> 26.8 us  [fused(): pl.pallas_call(functools.partial(fused_kernel, chans, bands), out_shape=p...]
where the time goes in v3:
time: 28.1 us; the launch traced here: 27.6 us
  Pallas kernels  26.8 us (95%)
  local copies, waits for them, and re-layouts  0.8 us (3%)
    pallas_call x1, Pallas kernels, fused(): pl.pallas_call(functools.partial(fused_kernel, chans, bands), out_shape=p...  26.8 us
    unnamed x1, local copies, waits for them, and re-layouts  0.8 us

profile of v3, /device:TPU:15, one launch (start us, length us, event | category | flops | bytes accessed | tf_op | source)
XLA Modules:
  0.0 27.6 jit_solution(2101864260640517166)
XLA Ops:
  0.0 26.8 %shard_map.46 = f32[4,256,128]{2,1,0:T(8,128)S(1)} custom-call(f32[4,256,128]{2,1,0:T(8,128)} %bitcast.11, f32[4,257]{1,0:T(4,128)} %row_hbm.1, f32[16,257]{1,0:T(8,128)} %column_hbm.1, f32[16,16]{1,0:T(8,128)} %mix_hbm.1), custom_call_target="tpu_custom_call" | custom-call | tf_op jit(solution)/shard_map/pallas_call | solution.py:411
  26.8 0.8 %copy.8 = f32[4,4,8192]{2,1,0:T(4,128)} copy(f32[4,4,8192]{2,1,0:T(4,128)S(1)} %bitcast.10) | data formatting | bytes 1048576

commit v4 on v1

--- a/solution.py
+++ b/solution.py
@@ -183,37 +183,39 @@
     for c in range(local_channels):
         pltpu.make_async_copy(x_hbm.at[c], x_inside.at[c], x_sem).start()
 
-    far = [jnp.where(left, half + k, half - 1 - k) for k in range(half)]
-    near = [jnp.where(left, 0, half) + (band + k) % half for k in range(1, half)]
-
-    def peers(to_band, own):
-        return [
-            ({"chan": chan ^ step, "band": to_band}, to_band * chans + (chan ^ step))
-            for step in range(1 if own else 0, chans)
-        ]
-
-    targets = [(to, peers(to, False)) for to in far + near] + [(band, peers(band, True))]
+    low = 2 * chan < chans
+    inner = jnp.logical_or(band == half - 1, band == half)
+    outer = jnp.logical_not(inner)
+    high = jnp.logical_not(low)
+    beside = band ^ 1
+    across = band ^ 3
+    first = jnp.where(inner, across, band ^ 2)
+    second = jnp.where(inner, band ^ 2, across)
+
+    def device(to_chan, to_band):
+        to_chan = jnp.int32(to_chan) if isinstance(to_chan, int) else to_chan
+        return {"chan": to_chan, "band": to_band}, to_band * chans + to_chan
+
+    def whole(to_band):
+        return [device(to_chan, to_band) for to_chan in range(chans)]
+
+    own = [device(chan ^ step, band) for step in range(1, chans)]
+    middle = chans // 2
 
     barrier = pltpu.get_barrier_semaphore()
-    greet = functools.partial(
-        pl.semaphore_signal, inc=1, device_id_type=pl.DeviceIdType.MESH
-    )
-
-    def greet_all(semaphore, upward):
-        for to, names in targets[:-1]:
-
-            @pl.when((to > band) if upward else (to < band))
-            def _():
-                for name, _slot in names:
-                    greet(semaphore, device_id=name)
-
-        for name, slot in targets[-1][1]:
-
-            @pl.when((slot > me) if upward else (slot < me))
-            def _():
-                greet(semaphore, device_id=name)
-
-    greet_all(barrier, True)
+    inner_ready, outer_ready, go_first, go_outer, go_all = (ready.at[k] for k in range(5))
+
+    def greet(semaphore, *names):
+        for name, _slot in names:
+            pl.semaphore_signal(
+                semaphore, inc=1, device_id=name, device_id_type=pl.DeviceIdType.MESH
+            )
+
+    @pl.when(inner)
+    def _():
+        pl.when(low)(lambda: greet(barrier, *whole(across)[:middle]))
+        greet(barrier, *whole(across)[middle:], *whole(beside))
+
     small_loads = [
         pltpu.make_async_copy(column_hbm, column_taps, small_sem.at[0]),
         pltpu.make_async_copy(mix_hbm, channel_mix, small_sem.at[1]),
@@ -226,20 +228,27 @@
         x_buf[c, 0:8, :] = edge
         x_buf[c, x_rows + 8 : x_rows + 16, :] = edge
 
-    @pl.when(me > 0)
-    def _():
-        pl.semaphore_wait(barrier, me)
-
-    greet_all(ready.at[band], False)
-
-    row_load.wait()
-    for c in range(local_channels):
-        tables[c, 0], tables[c, 1] = split(filter_table(row_taps[c : c + 1, :]))
-    pltpu.make_async_copy(x_hbm, x_inside, x_sem).wait()
-
-    def filter_band(which):
+    def meet():
+        pl.semaphore_wait(barrier, jnp.where(jnp.logical_and(inner, low), middle, chans))
+
+        @pl.when(jnp.logical_and(inner, high))
+        def _():
+            greet(inner_ready, *whole(across)[:middle])
+
+        @pl.when(outer)
+        def _():
+            greet(outer_ready, *whole(beside))
+
+    meet_first = jnp.logical_and(high, jnp.logical_not(left))
+    pl.when(meet_first)(meet)
+
+    def make_tables(channels):
+        for c in channels:
+            tables[c, 0:LANES], tables[c, LANES:] = split(filter_table(row_taps[c : c + 1, :]))
+
+    def filter_band(which, channels):
         start = pl.multiple_of(which * band_rows, 8)
-        for c in range(local_channels):
+        for c in channels:
             wide = x_buf[c, pl.ds(start, band_rows + 16), :]
             window = jnp.concatenate(
                 [
@@ -248,45 +257,99 @@
                 ],
                 axis=1,
             )
-            filtered = product(split(window), (tables[c, 0], tables[c, 1]), ((1,), (1,)))
-            for device in range(chans):
+            both = lax.dot_general(
+                jnp.concatenate(split(window), axis=0),
+                tables[c],
+                (((1,), (1,)), ((), ())),
+                preferred_element_type=jnp.float32,
+            )
+            filtered = both[:band_rows, :LANES] + (
+                both[band_rows:, :LANES] + both[:band_rows, LANES:]
+            )
+            for to in range(chans):
                 for tile in range(tiles):
-                    at = (device * tiles + tile) * local_rows
+                    at = (to * tiles + tile) * local_rows
                     send_one[
-                        which * chans + device,
+                        which * chans + to,
                         tile,
                         c * local_rows : (c + 1) * local_rows,
                         :,
                     ] = filtered[at : at + local_rows, :]
 
     step = tiles // CHUNKS
-
-    def copy_one(chunk, name, slot):
-        part = pl.ds(chunk * step, step)
-        return pltpu.make_async_remote_copy(
-            src_ref=send_one.at[slot, part],
-            dst_ref=recv_one.at[part, me],
-            send_sem=send_sem.at[0],
-            recv_sem=recv_one_sem.at[chunk],
-            device_id=name,
-            device_id_type=pl.DeviceIdType.MESH,
-        )
-
-    for to, names in targets:
-        own = to is band
-        filter_band(to)
-        above = (chans - 1 - chan) if own else chans
-
-        @pl.when((above > 0) if own else (to > band))
-        def _():
-            pl.semaphore_wait(ready.at[to], above)
-
+    block = local_channels * local_rows
+    every = (0, block)
+
+    def send(chunk, names, rows=every):
+        part, lines = pl.ds(chunk * step, step), pl.ds(rows[0], rows[1])
         for name, slot in names:
-            copy_one(0, name, slot).start()
+            pltpu.make_async_remote_copy(
+                src_ref=send_one.at[slot, part, lines],
+                dst_ref=recv_one.at[part, me, lines],
+                send_sem=send_sem.at[0],
+                recv_sem=recv_one_sem.at[chunk],
+                device_id=name,
+                device_id_type=pl.DeviceIdType.MESH,
+            ).start()
+
+    row_load.wait()
+    near, far = whole(first)[:middle], whole(first)[middle:]
+    both_high = jnp.logical_and(inner, high)
+    both_low = jnp.logical_and(inner, low)
+    for piece in range(2):
+        channels = range(piece * local_channels // 2, (piece + 1) * local_channels // 2)
+        rows = (piece * block // 2, block // 2)
+        make_tables(channels)
+        if piece == 0:
+            pltpu.make_async_copy(x_hbm, x_inside, x_sem).wait()
+        filter_band(first, channels)
+        if piece == 0:
+            pl.when(jnp.logical_not(meet_first))(meet)
+        pl.when(inner)(lambda: send(0, near, rows))
+        pl.when(both_high)(lambda: send(0, far, rows))
     for chunk in range(1, CHUNKS):
-        for to, names in targets:
-            for name, slot in names:
-                copy_one(chunk, name, slot).start()
+        pl.when(inner)(lambda: send(chunk, near))
+        pl.when(both_high)(lambda: send(chunk, far))
+    for to in (beside, second, band):
+        filter_band(to, range(local_channels))
+
+    @pl.when(both_low)
+    def _():
+        pl.semaphore_wait(inner_ready, middle)
+        for chunk in range(CHUNKS):
+            send(chunk, far)
+
+    @pl.when(inner)
+    def _():
+        pl.semaphore_wait(outer_ready, chans)
+        greet(go_first, device(chan, beside))
+        greet(go_outer, device(chan, across))
+
+    pl.when(inner)(lambda: send(0, whole(beside)))
+
+    @pl.when(outer)
+    def _():
+        pl.semaphore_wait(go_first, 1)
+        send(0, near + far)
+        send(0, whole(beside))
+        send(0, own)
+
+    @pl.when(inner)
+    def _():
+        pl.semaphore_wait(go_outer, 1)
+        greet(go_all, device(chan, beside))
+
+    @pl.when(outer)
+    def _():
+        pl.semaphore_wait(go_all, 1)
+
+    send(0, whole(second))
+    pl.when(inner)(lambda: send(0, own))
+    for chunk in range(1, CHUNKS):
+        pl.when(outer)(lambda: send(chunk, near + far))
+        send(chunk, whole(second))
+        send(chunk, whole(beside))
+        send(chunk, own)
     recv_one[:, me] = send_one[me]
 
     for load in small_loads:
@@ -298,8 +361,8 @@
 
     rows = step * local_rows
 
-    def copy_two(chunk, name, slot):
-        return pltpu.make_async_remote_copy(
+    def back(chunk, name, slot):
+        pltpu.make_async_remote_copy(
             src_ref=send_two.at[slot, :, pl.ds(chunk * rows, rows)],
             dst_ref=out_ref.at[
                 :, pl.ds(pl.multiple_of(me * block_rows + chunk * rows, 8), rows)
@@ -308,7 +371,27 @@
             recv_sem=recv_two_sem,
             device_id=name,
             device_id_type=pl.DeviceIdType.MESH,
-        )
+        ).start()
+
+    late = band == half
+    prompt = jnp.logical_not(late)
+
+    def send_back(chunk):
+        for part in range(2):
+            for k in range(half):
+                for name, slot in whole(jnp.where(left, half + k, k))[
+                    part * middle : (part + 1) * middle
+                ]:
+                    if part == 0 or k == 0:
+                        back(chunk, name, slot)
+                    elif chunk < CHUNKS - 1:
+                        pl.when(prompt)(functools.partial(back, chunk, name, slot))
+                    else:
+                        for held in range(chunk):
+                            pl.when(late)(functools.partial(back, held, name, slot))
+                        back(chunk, name, slot)
+        for name, slot in whole(beside) + own:
+            back(chunk, name, slot)
 
     for chunk in range(CHUNKS):
         part = pl.ds(chunk * step, step)
@@ -322,18 +405,16 @@
             axis=1,
         )
         mixed = product((mixing[0], mixing[1]), split(columns), ((1,), (0,)))
-        for device in range(devices):
+        for to_device in range(devices):
             for c in range(local_channels):
-                at = (device * local_channels + c) * local_rows
+                at = (to_device * local_channels + c) * local_rows
                 for tile in range(step):
                     to = (chunk * step + tile) * local_rows
-                    send_two[device, c, to : to + local_rows, :] = mixed[
+                    send_two[to_device, c, to : to + local_rows, :] = mixed[
                         at : at + local_rows, tile * LANES : (tile + 1) * LANES
                     ]
         there = pl.ds(pl.multiple_of(me * block_rows + chunk * rows, 8), rows)
-        for _to, names in targets:
-            for name, slot in names:
-                copy_two(chunk, name, slot).start()
+        send_back(chunk)
         out_ref[:, there, :] = send_two[me, :, chunk * rows : (chunk + 1) * rows, :]
 
     sent = send_one.at[others]
@@ -365,12 +446,12 @@
             pltpu.VMEM(row_taps.shape, jnp.float32),
             pltpu.VMEM(column_taps.shape, jnp.float32),
             pltpu.VMEM(channel_mix.shape, jnp.float32),
-            pltpu.VMEM((local_channels, 2, LANES, 3 * LANES), jnp.bfloat16),
+            pltpu.VMEM((local_channels, 2 * LANES, 3 * LANES), jnp.bfloat16),
             pltpu.VMEM((devices, tiles, block, LANES), jnp.float32),
             pltpu.VMEM((tiles, devices, block, LANES), jnp.float32),
             pltpu.VMEM((devices, local_channels, tiles * local_rows, LANES), jnp.float32),
             pltpu.VMEM((2, devices * block, devices * block), jnp.bfloat16),
-            pltpu.SemaphoreType.REGULAR((bands,)),
+            pltpu.SemaphoreType.REGULAR((5,)),
             dma,
             dma,
             dma((2,)),
@@ -394,14 +475,14 @@
     margin = (row_taps.shape[1] - 1) // 2
     fits = (
         power_of_two(chans)
-        and power_of_two(bands)
-        and bands > 1
+        and chans > 1
+        and bands == 4
         and width % (devices * LANES * CHUNKS) == 0
         and margin == LANES
         and column_taps.shape[1] == row_taps.shape[1]
         and local_rows == 4
+        and local_channels * local_rows % 16 == 0
         and local_rows * bands <= margin
-        and local_channels * local_rows % 8 == 0
         and width // (devices * LANES * CHUNKS) * local_rows % 8 == 0
         and devices * local_channels * local_rows <= 512
     )

time: 30.8 us -> 27.8 us (0.903)
  the two profiles are of different devices: /device:TPU:0 before, /device:TPU:15 now
where the time goes in v4:
time: 27.8 us; the launch traced here: 27.5 us
  Pallas kernels  26.7 us (96%)
  local copies, waits for them, and re-layouts  0.8 us (3%)
    pallas_call x1, Pallas kernels, fused(): pl.pallas_call(functools.partial(fused_kernel, chans, bands), out_shape=p...  26.7 us
    unnamed x1, local copies, waits for them, and re-layouts  0.8 us

profile of v4, /device:TPU:15, one launch (start us, length us, event | category | flops | bytes accessed | tf_op | source)
XLA Modules:
  0.0 27.5 jit_solution(1103596923799456342)
XLA Ops:
  0.0 26.7 %shard_map.46 = f32[4,256,128]{2,1,0:T(8,128)S(1)} custom-call(f32[4,256,128]{2,1,0:T(8,128)} %bitcast.11, f32[4,257]{1,0:T(4,128)} %row_hbm.1, f32[16,257]{1,0:T(8,128)} %column_hbm.1, f32[16,16]{1,0:T(8,128)} %mix_hbm.1), custom_call_target="tpu_custom_call" | custom-call | tf_op jit(solution)/shard_map/pallas_call | solution.py:439
  26.7 0.8 %copy.8 = f32[4,4,8192]{2,1,0:T(4,128)} copy(f32[4,4,8192]{2,1,0:T(4,128)S(1)} %bitcast.10) | data formatting | bytes 1048576

commit v5 on v4

--- a/solution.py
+++ b/solution.py
@@ -164,7 +164,7 @@
     chans, bands, x_hbm, row_hbm, column_hbm, mix_hbm, out_ref,
     x_buf, row_taps, column_taps, channel_mix, tables,
     send_one, recv_one, send_two, mixing,
-    ready, x_sem, row_sem, small_sem, send_sem, recv_one_sem, recv_two_sem,
+    ready, x_sem, row_sem, send_sem, recv_one_sem, recv_two_sem,
 ):
     local_channels, x_rows, _ = x_hbm.shape
     devices, _, block_rows, _ = send_two.shape
@@ -203,7 +203,9 @@
     middle = chans // 2
 
     barrier = pltpu.get_barrier_semaphore()
-    inner_ready, outer_ready, go_first, go_outer, go_all = (ready.at[k] for k in range(5))
+    inner_ready = ready.at[0]
+    outer_ready = go_first = ready.at[1]
+    go_outer = go_all = ready.at[2]
 
     def greet(semaphore, *names):
         for name, _slot in names:
@@ -215,13 +217,6 @@
     def _():
         pl.when(low)(lambda: greet(barrier, *whole(across)[:middle]))
         greet(barrier, *whole(across)[middle:], *whole(beside))
-
-    small_loads = [
-        pltpu.make_async_copy(column_hbm, column_taps, small_sem.at[0]),
-        pltpu.make_async_copy(mix_hbm, channel_mix, small_sem.at[1]),
-    ]
-    for load in small_loads:
-        load.start()
 
     edge = jnp.zeros((8, LANES), jnp.float32)
     for c in range(local_channels):
@@ -307,6 +302,12 @@
             pl.when(jnp.logical_not(meet_first))(meet)
         pl.when(inner)(lambda: send(0, near, rows))
         pl.when(both_high)(lambda: send(0, far, rows))
+    small_loads = [
+        pltpu.make_async_copy(column_hbm, column_taps, row_sem),
+        pltpu.make_async_copy(mix_hbm, channel_mix, x_sem),
+    ]
+    for load in small_loads:
+        load.start()
     for chunk in range(1, CHUNKS):
         pl.when(inner)(lambda: send(chunk, near))
         pl.when(both_high)(lambda: send(chunk, far))
@@ -377,8 +378,8 @@
     prompt = jnp.logical_not(late)
 
     def send_back(chunk):
-        for part in range(2):
-            for k in range(half):
+        for part, k in ((0, 0), (1, 0), (0, 1), (1, 1)):
+            if True:
                 for name, slot in whole(jnp.where(left, half + k, k))[
                     part * middle : (part + 1) * middle
                 ]:
@@ -451,10 +452,9 @@
             pltpu.VMEM((tiles, devices, block, LANES), jnp.float32),
             pltpu.VMEM((devices, local_channels, tiles * local_rows, LANES), jnp.float32),
             pltpu.VMEM((2, devices * block, devices * block), jnp.bfloat16),
-            pltpu.SemaphoreType.REGULAR((5,)),
+            pltpu.SemaphoreType.REGULAR((3,)),
             dma,
             dma,
-            dma((2,)),
             dma((2,)),
             dma((CHUNKS,)),
             dma,

time: 27.8 us -> 27.6 us (level)
  no operation moved by 1% of the time
where the time goes in v5:
time: 27.6 us; the launch traced here: 27.4 us
  Pallas kernels  26.6 us (96%)
  local copies, waits for them, and re-layouts  0.8 us (3%)
    pallas_call x1, Pallas kernels, fused(): pl.pallas_call(functools.partial(fused_kernel, chans, bands), out_shape=p...  26.6 us
    unnamed x1, local copies, waits for them, and re-layouts  0.8 us

profile of v5, /device:TPU:15, one launch (start us, length us, event | category | flops | bytes accessed | tf_op | source)
XLA Modules:
  0.0 27.4 jit_solution(17132440257897755946)
XLA Ops:
  0.0 26.6 %shard_map.46 = f32[4,256,128]{2,1,0:T(8,128)S(1)} custom-call(f32[4,256,128]{2,1,0:T(8,128)} %bitcast.11, f32[4,257]{1,0:T(4,128)} %row_hbm.1, f32[16,257]{1,0:T(8,128)} %column_hbm.1, f32[16,16]{1,0:T(8,128)} %mix_hbm.1), custom_call_target="tpu_custom_call" | custom-call | tf_op jit(solution)/shard_map/pallas_call | solution.py:440
  26.6 0.8 %copy.8 = f32[4,4,8192]{2,1,0:T(4,128)} copy(f32[4,4,8192]{2,1,0:T(4,128)S(1)} %bitcast.10) | data formatting | bytes 1048576

commit v6 on v5

--- a/solution.py
+++ b/solution.py
@@ -216,6 +216,8 @@
     @pl.when(inner)
     def _():
         pl.when(low)(lambda: greet(barrier, *whole(across)[:middle]))
+        vouched = jnp.logical_and(left, high)
+        pl.when(vouched)(lambda: greet(barrier, *whole(band)[:middle]))
         greet(barrier, *whole(across)[middle:], *whole(beside))
 
     edge = jnp.zeros((8, LANES), jnp.float32)
@@ -223,12 +225,19 @@
         x_buf[c, 0:8, :] = edge
         x_buf[c, x_rows + 8 : x_rows + 16, :] = edge
 
+    right_low = jnp.logical_and(jnp.logical_and(inner, low), jnp.logical_not(left))
+    left_low = jnp.logical_and(jnp.logical_and(inner, low), left)
+
     def meet():
-        pl.semaphore_wait(barrier, jnp.where(jnp.logical_and(inner, low), middle, chans))
-
-        @pl.when(jnp.logical_and(inner, high))
+        pl.semaphore_wait(barrier, jnp.where(right_low, middle, chans))
+
+        @pl.when(jnp.logical_and(inner, jnp.logical_not(left)))
         def _():
-            greet(inner_ready, *whole(across)[:middle])
+            pl.when(high)(lambda: greet(inner_ready, *whole(across)[:middle]))
+
+        @pl.when(jnp.logical_and(inner, left))
+        def _():
+            pl.when(low)(lambda: greet(inner_ready, device(chan, across)))
 
         @pl.when(outer)
         def _():
@@ -290,7 +299,6 @@
     row_load.wait()
     near, far = whole(first)[:middle], whole(first)[middle:]
     both_high = jnp.logical_and(inner, high)
-    both_low = jnp.logical_and(inner, low)
     for piece in range(2):
         channels = range(piece * local_channels // 2, (piece + 1) * local_channels // 2)
         rows = (piece * block // 2, block // 2)
@@ -311,10 +319,17 @@
     for chunk in range(1, CHUNKS):
         pl.when(inner)(lambda: send(chunk, near))
         pl.when(both_high)(lambda: send(chunk, far))
+
+    @pl.when(right_low)
+    def _():
+        pl.semaphore_wait(inner_ready, 1)
+        for chunk in range(CHUNKS):
+            send(chunk, far)
+
     for to in (beside, second, band):
         filter_band(to, range(local_channels))
 
-    @pl.when(both_low)
+    @pl.when(left_low)
     def _():
         pl.semaphore_wait(inner_ready, middle)
         for chunk in range(CHUNKS):
@@ -377,22 +392,25 @@
     late = band == half
     prompt = jnp.logical_not(late)
 
-    def send_back(chunk):
-        for part, k in ((0, 0), (1, 0), (0, 1), (1, 1)):
-            if True:
-                for name, slot in whole(jnp.where(left, half + k, k))[
-                    part * middle : (part + 1) * middle
-                ]:
-                    if part == 0 or k == 0:
-                        back(chunk, name, slot)
-                    elif chunk < CHUNKS - 1:
-                        pl.when(prompt)(functools.partial(back, chunk, name, slot))
-                    else:
-                        for held in range(chunk):
-                            pl.when(late)(functools.partial(back, held, name, slot))
-                        back(chunk, name, slot)
+    def send_near(chunk):
         for name, slot in whole(beside) + own:
             back(chunk, name, slot)
+
+    def send_back(chunk):
+        pl.when(left)(functools.partial(send_near, chunk))
+        for k in range(half):
+            to = jnp.where(left, half + k, k)
+            crossed = [device(chan ^ step, to) for step in reversed(range(chans))]
+            for at, (name, slot) in enumerate(crossed if k else whole(to)):
+                if k == 0 or at not in (2, 3):
+                    back(chunk, name, slot)
+                elif chunk < CHUNKS - 1:
+                    pl.when(prompt)(functools.partial(back, chunk, name, slot))
+                else:
+                    for held in range(chunk):
+                        pl.when(late)(functools.partial(back, held, name, slot))
+                    back(chunk, name, slot)
+        pl.when(jnp.logical_not(left))(functools.partial(send_near, chunk))
 
     for chunk in range(CHUNKS):
         part = pl.ds(chunk * step, step)

time: 27.6 us -> 27.5 us (level)
  no operation moved by 1% of the time
where the time goes in v6:
time: 27.5 us; the launch traced here: 27.2 us
  Pallas kernels  26.4 us (96%)
  local copies, waits for them, and re-layouts  0.8 us (3%)
    pallas_call x1, Pallas kernels, fused(): pl.pallas_call(functools.partial(fused_kernel, chans, bands), out_shape=p...  26.4 us
    unnamed x1, local copies, waits for them, and re-layouts  0.8 us

profile of v6, /device:TPU:15, one launch (start us, length us, event | category | flops | bytes accessed | tf_op | source)
XLA Modules:
  0.0 27.2 jit_solution(11576999215941576510)
XLA Ops:
  0.0 26.4 %shard_map.46 = f32[4,256,128]{2,1,0:T(8,128)S(1)} custom-call(f32[4,256,128]{2,1,0:T(8,128)} %bitcast.11, f32[4,257]{1,0:T(4,128)} %row_hbm.1, f32[16,257]{1,0:T(8,128)} %column_hbm.1, f32[16,16]{1,0:T(8,128)} %mix_hbm.1), custom_call_target="tpu_custom_call" | custom-call | tf_op jit(solution)/shard_map/pallas_call | solution.py:458
  26.4 0.8 %copy.8 = f32[4,4,8192]{2,1,0:T(4,128)} copy(f32[4,4,8192]{2,1,0:T(4,128)S(1)} %bitcast.10) | data formatting | bytes 1048576

commit v7 on v6

--- a/solution.py
+++ b/solution.py
@@ -181,7 +181,9 @@
     row_load.start()
     x_inside = x_buf.at[:, pl.ds(8, x_rows)]
     for c in range(local_channels):
-        pltpu.make_async_copy(x_hbm.at[c], x_inside.at[c], x_sem).start()
+        pltpu.make_async_copy(
+            x_hbm.at[c], x_inside.at[c], x_sem.at[2 * c // local_channels]
+        ).start()
 
     low = 2 * chan < chans
     inner = jnp.logical_or(band == half - 1, band == half)
@@ -220,6 +222,12 @@
         pl.when(vouched)(lambda: greet(barrier, *whole(band)[:middle]))
         greet(barrier, *whole(across)[middle:], *whole(beside))
 
+    mixing[...] = jnp.zeros(mixing.shape, mixing.dtype)
+    span = devices // local_channels
+    for lap in range(3):
+        send_two[pl.ds(lap % local_channels * span, span)] = lax.dot_general(
+            mixing[0], mixing[1], (((1,), (1,)), ((), ())), preferred_element_type=jnp.float32
+        )[:, :LANES].reshape(span, *send_two.shape[1:])
     edge = jnp.zeros((8, LANES), jnp.float32)
     for c in range(local_channels):
         x_buf[c, 0:8, :] = edge
@@ -303,22 +311,20 @@
         channels = range(piece * local_channels // 2, (piece + 1) * local_channels // 2)
         rows = (piece * block // 2, block // 2)
         make_tables(channels)
-        if piece == 0:
-            pltpu.make_async_copy(x_hbm, x_inside, x_sem).wait()
+        loaded = x_inside.at[pl.ds(channels[0], len(channels))]
+        pltpu.make_async_copy(loaded, loaded, x_sem.at[piece]).wait()
         filter_band(first, channels)
         if piece == 0:
             pl.when(jnp.logical_not(meet_first))(meet)
-        pl.when(inner)(lambda: send(0, near, rows))
-        pl.when(both_high)(lambda: send(0, far, rows))
+        for chunk in range(CHUNKS):
+            pl.when(inner)(lambda: send(chunk, near, rows))
+            pl.when(both_high)(lambda: send(chunk, far, rows))
     small_loads = [
         pltpu.make_async_copy(column_hbm, column_taps, row_sem),
-        pltpu.make_async_copy(mix_hbm, channel_mix, x_sem),
+        pltpu.make_async_copy(mix_hbm, channel_mix, x_sem.at[0]),
     ]
     for load in small_loads:
         load.start()
-    for chunk in range(1, CHUNKS):
-        pl.when(inner)(lambda: send(chunk, near))
-        pl.when(both_high)(lambda: send(chunk, far))
 
     @pl.when(right_low)
     def _():
@@ -390,7 +396,6 @@
         ).start()
 
     late = band == half
-    prompt = jnp.logical_not(late)
 
     def send_near(chunk):
         for name, slot in whole(beside) + own:
@@ -402,13 +407,14 @@
             to = jnp.where(left, half + k, k)
             crossed = [device(chan ^ step, to) for step in reversed(range(chans))]
             for at, (name, slot) in enumerate(crossed if k else whole(to)):
-                if k == 0 or at not in (2, 3):
+                hold = jnp.logical_and(late, low) if at < 2 else late
+                if k == 0:
                     back(chunk, name, slot)
                 elif chunk < CHUNKS - 1:
-                    pl.when(prompt)(functools.partial(back, chunk, name, slot))
+                    pl.when(jnp.logical_not(hold))(functools.partial(back, chunk, name, slot))
                 else:
                     for held in range(chunk):
-                        pl.when(late)(functools.partial(back, held, name, slot))
+                        pl.when(hold)(functools.partial(back, held, name, slot))
                     back(chunk, name, slot)
         pl.when(jnp.logical_not(left))(functools.partial(send_near, chunk))
 
@@ -471,7 +477,7 @@
             pltpu.VMEM((devices, local_channels, tiles * local_rows, LANES), jnp.float32),
             pltpu.VMEM((2, devices * block, devices * block), jnp.bfloat16),
             pltpu.SemaphoreType.REGULAR((3,)),
-            dma,
+            dma((2,)),
             dma,
             dma((2,)),
             dma((CHUNKS,)),

time: 27.5 us -> 27.3 us (level)
  no operation moved by 1% of the time
where the time goes in v7:
time: 27.3 us; the launch traced here: 27 us
  Pallas kernels  26.2 us (96%)
  local copies, waits for them, and re-layouts  0.8 us (3%)
    pallas_call x1, Pallas kernels, fused(): pl.pallas_call(functools.partial(fused_kernel, chans, bands), out_shape=p...  26.2 us
    unnamed x1, local copies, waits for them, and re-layouts  0.8 us

profile of v7, /device:TPU:15, one launch (start us, length us, event | category | flops | bytes accessed | tf_op | source)
XLA Modules:
  0.0 27.0 jit_solution(17069765008451130165)
XLA Ops:
  0.0 26.2 %shard_map.46 = f32[4,256,128]{2,1,0:T(8,128)S(1)} custom-call(f32[4,256,128]{2,1,0:T(8,128)} %bitcast.11, f32[4,257]{1,0:T(4,128)} %row_hbm.1, f32[16,257]{1,0:T(8,128)} %column_hbm.1, f32[16,16]{1,0:T(8,128)} %mix_hbm.1), custom_call_target="tpu_custom_call" | custom-call | tf_op jit(solution)/shard_map/pallas_call | solution.py:464
  26.2 0.8 %copy.8 = f32[4,4,8192]{2,1,0:T(4,128)} copy(f32[4,4,8192]{2,1,0:T(4,128)S(1)} %bitcast.10) | data formatting | bytes 1048576

commit v8 on v7

--- a/solution.py
+++ b/solution.py
@@ -396,13 +396,15 @@
         ).start()
 
     late = band == half
+    near_first = jnp.logical_or(left, band > half)
 
     def send_near(chunk):
         for name, slot in whole(beside) + own:
             back(chunk, name, slot)
 
     def send_back(chunk):
-        pl.when(left)(functools.partial(send_near, chunk))
+        early = near_first if chunk else left
+        pl.when(early)(functools.partial(send_near, chunk))
         for k in range(half):
             to = jnp.where(left, half + k, k)
             crossed = [device(chan ^ step, to) for step in reversed(range(chans))]
@@ -416,7 +418,7 @@
                     for held in range(chunk):
                         pl.when(hold)(functools.partial(back, held, name, slot))
                     back(chunk, name, slot)
-        pl.when(jnp.logical_not(left))(functools.partial(send_near, chunk))
+        pl.when(jnp.logical_not(early))(functools.partial(send_near, chunk))
 
     for chunk in range(CHUNKS):
         part = pl.ds(chunk * step, step)

time: 27.3 us -> 27.3 us (level)
  no operation moved by 1% of the time
where the time goes in v8:
time: 27.3 us; the launch traced here: 27 us
  Pallas kernels  26.2 us (96%)
  local copies, waits for them, and re-layouts  0.8 us (3%)
    pallas_call x1, Pallas kernels, fused(): pl.pallas_call(functools.partial(fused_kernel, chans, bands), out_shape=p...  26.2 us
    unnamed x1, local copies, waits for them, and re-layouts  0.8 us

profile of v8, /device:TPU:15, one launch (start us, length us, event | category | flops | bytes accessed | tf_op | source)
XLA Modules:
  0.0 27.0 jit_solution(10312811323842262609)
XLA Ops:
  0.0 26.2 %shard_map.46 = f32[4,256,128]{2,1,0:T(8,128)S(1)} custom-call(f32[4,256,128]{2,1,0:T(8,128)} %bitcast.11, f32[4,257]{1,0:T(4,128)} %row_hbm.1, f32[16,257]{1,0:T(8,128)} %column_hbm.1, f32[16,16]{1,0:T(8,128)} %mix_hbm.1), custom_call_target="tpu_custom_call" | custom-call | tf_op jit(solution)/shard_map/pallas_call | solution.py:466
  26.2 0.8 %copy.8 = f32[4,4,8192]{2,1,0:T(4,128)} copy(f32[4,4,8192]{2,1,0:T(4,128)S(1)} %bitcast.10) | data formatting | bytes 1048576

commit v9 on v8

--- a/solution.py
+++ b/solution.py
@@ -368,9 +368,10 @@
     send(0, whole(second))
     pl.when(inner)(lambda: send(0, own))
     for chunk in range(1, CHUNKS):
+        pl.when(outer)(lambda: send(chunk, whole(beside)))
         pl.when(outer)(lambda: send(chunk, near + far))
         send(chunk, whole(second))
-        send(chunk, whole(beside))
+        pl.when(inner)(lambda: send(chunk, whole(beside)))
         send(chunk, own)
     recv_one[:, me] = send_one[me]
 

time: 27.3 us -> 27.3 us (level)
  the two profiles are of different devices: /device:TPU:15 before, /device:TPU:8 now
where the time goes in v9:
time: 27.3 us; the launch traced here: 27.1 us
  Pallas kernels  26.3 us (96%)
  local copies, waits for them, and re-layouts  0.8 us (3%)
    pallas_call x1, Pallas kernels, fused(): pl.pallas_call(functools.partial(fused_kernel, chans, bands), out_shape=p...  26.3 us
    unnamed x1, local copies, waits for them, and re-layouts  0.8 us

profile of v9, /device:TPU:8, one launch (start us, length us, event | category | flops | bytes accessed | tf_op | source)
XLA Modules:
  0.0 27.1 jit_solution(8049671737542488192)
XLA Ops:
  0.0 26.3 %shard_map.46 = f32[4,256,128]{2,1,0:T(8,128)S(1)} custom-call(f32[4,256,128]{2,1,0:T(8,128)} %bitcast.11, f32[4,257]{1,0:T(4,128)} %row_hbm.1, f32[16,257]{1,0:T(8,128)} %column_hbm.1, f32[16,16]{1,0:T(8,128)} %mix_hbm.1), custom_call_target="tpu_custom_call" | custom-call | tf_op jit(solution)/shard_map/pallas_call | solution.py:467
  26.3 0.8 %copy.8 = f32[4,4,8192]{2,1,0:T(4,128)} copy(f32[4,4,8192]{2,1,0:T(4,128)S(1)} %bitcast.10) | data formatting | bytes 1048576

commit v10 on v9

--- a/solution.py
+++ b/solution.py
@@ -408,7 +408,7 @@
         pl.when(early)(functools.partial(send_near, chunk))
         for k in range(half):
             to = jnp.where(left, half + k, k)
-            crossed = [device(chan ^ step, to) for step in reversed(range(chans))]
+            crossed = [device(chan ^ jnp.where(low, a, b), to) for a, b in zip([1, 0, 3, 2], [3, 2, 1, 0])]
             for at, (name, slot) in enumerate(crossed if k else whole(to)):
                 hold = jnp.logical_and(late, low) if at < 2 else late
                 if k == 0:

time: 27.3 us -> 27.2 us (level)
  the two profiles are of different devices: /device:TPU:8 before, /device:TPU:15 now
where the time goes in v10:
time: 27.2 us; the launch traced here: 26.9 us
  Pallas kernels  26.1 us (96%)
  local copies, waits for them, and re-layouts  0.8 us (3%)
    pallas_call x1, Pallas kernels, fused(): pl.pallas_call(functools.partial(fused_kernel, chans, bands), out_shape=p...  26.1 us
    unnamed x1, local copies, waits for them, and re-layouts  0.8 us

profile of v10, /device:TPU:15, one launch (start us, length us, event | category | flops | bytes accessed | tf_op | source)
XLA Modules:
  0.0 26.9 jit_solution(15469672936378784662)
XLA Ops:
  0.0 26.1 %shard_map.46 = f32[4,256,128]{2,1,0:T(8,128)S(1)} custom-call(f32[4,256,128]{2,1,0:T(8,128)} %bitcast.11, f32[4,257]{1,0:T(4,128)} %row_hbm.1, f32[16,257]{1,0:T(8,128)} %column_hbm.1, f32[16,16]{1,0:T(8,128)} %mix_hbm.1), custom_call_target="tpu_custom_call" | custom-call | tf_op jit(solution)/shard_map/pallas_call | solution.py:467
  26.1 0.8 %copy.8 = f32[4,4,8192]{2,1,0:T(4,128)} copy(f32[4,4,8192]{2,1,0:T(4,128)S(1)} %bitcast.10) | data formatting | bytes 1048576

commit v11 on v10

--- a/solution.py
+++ b/solution.py
@@ -410,7 +410,7 @@
             to = jnp.where(left, half + k, k)
             crossed = [device(chan ^ jnp.where(low, a, b), to) for a, b in zip([1, 0, 3, 2], [3, 2, 1, 0])]
             for at, (name, slot) in enumerate(crossed if k else whole(to)):
-                hold = jnp.logical_and(late, low) if at < 2 else late
+                hold = jnp.logical_and(late, low)
                 if k == 0:
                     back(chunk, name, slot)
                 elif chunk < CHUNKS - 1:

time: 27.2 us -> 28.4 us (1.044)
  the two profiles are of different devices: /device:TPU:15 before, /device:TPU:0 now
where the time goes in v11:
time: 28.4 us; the launch traced here: 28.3 us
  Pallas kernels  27.5 us (97%)
  local copies, waits for them, and re-layouts  0.8 us (3%)
    pallas_call x1, Pallas kernels, fused(): pl.pallas_call(functools.partial(fused_kernel, chans, bands), out_shape=p...  27.5 us
    unnamed x1, local copies, waits for them, and re-layouts  0.8 us

profile of v11, /device:TPU:0, one launch (start us, length us, event | category | flops | bytes accessed | tf_op | source)
XLA Modules:
  0.0 28.3 jit_solution(1958102621818916979)
XLA Ops:
  0.0 27.5 %shard_map.46 = f32[4,256,128]{2,1,0:T(8,128)S(1)} custom-call(f32[4,256,128]{2,1,0:T(8,128)} %bitcast.11, f32[4,257]{1,0:T(4,128)} %row_hbm.1, f32[16,257]{1,0:T(8,128)} %column_hbm.1, f32[16,16]{1,0:T(8,128)} %mix_hbm.1), custom_call_target="tpu_custom_call" | custom-call | tf_op jit(solution)/shard_map/pallas_call | solution.py:467
  27.5 0.8 %copy.8 = f32[4,4,8192]{2,1,0:T(4,128)} copy(f32[4,4,8192]{2,1,0:T(4,128)S(1)} %bitcast.10) | data formatting | bytes 1048576

commit v12 on v10

--- a/solution.py
+++ b/solution.py
@@ -408,7 +408,7 @@
         pl.when(early)(functools.partial(send_near, chunk))
         for k in range(half):
             to = jnp.where(left, half + k, k)
-            crossed = [device(chan ^ jnp.where(low, a, b), to) for a, b in zip([1, 0, 3, 2], [3, 2, 1, 0])]
+            crossed = [device(chan ^ jnp.where(low, a, b), to) for a, b in zip([1, 0, 3, 2], [3, 1, 2, 0])]
             for at, (name, slot) in enumerate(crossed if k else whole(to)):
                 hold = jnp.logical_and(late, low) if at < 2 else late
                 if k == 0:

time: 27.2 us -> 27.7 us (1.018)
  the two profiles are of different devices: /device:TPU:15 before, /device:TPU:8 now
where the time goes in v12:
time: 27.7 us; the launch traced here: 27.5 us
  Pallas kernels  26.7 us (96%)
  local copies, waits for them, and re-layouts  0.8 us (3%)
    pallas_call x1, Pallas kernels, fused(): pl.pallas_call(functools.partial(fused_kernel, chans, bands), out_shape=p...  26.7 us
    unnamed x1, local copies, waits for them, and re-layouts  0.8 us

profile of v12, /device:TPU:8, one launch (start us, length us, event | category | flops | bytes accessed | tf_op | source)
XLA Modules:
  0.0 27.5 jit_solution(577225057704477100)
XLA Ops:
  0.0 26.7 %shard_map.46 = f32[4,256,128]{2,1,0:T(8,128)S(1)} custom-call(f32[4,256,128]{2,1,0:T(8,128)} %bitcast.11, f32[4,257]{1,0:T(4,128)} %row_hbm.1, f32[16,257]{1,0:T(8,128)} %column_hbm.1, f32[16,16]{1,0:T(8,128)} %mix_hbm.1), custom_call_target="tpu_custom_call" | custom-call | tf_op jit(solution)/shard_map/pallas_call | solution.py:467
  26.7 0.8 %copy.8 = f32[4,4,8192]{2,1,0:T(4,128)} copy(f32[4,4,8192]{2,1,0:T(4,128)S(1)} %bitcast.10) | data formatting | bytes 1048576
